TPU v7x, 16 devices: a whole 2x2x2 slice. The times are simulated.
16 devices in a mesh: local: 4 (over z, y), data: 4 (over x, core).
Axes of the slice: x: 2, y: 2, z: 2, core: 2. Of those that a mesh axis runs over, the one named last changes fastest.
Arguments:
- tokens: bfloat16 [32768, 1024], P(('data', 'local'))
- cotangent: bfloat16 [32768, 1024], P(('data', 'local'))
- w_up: bfloat16 [4, 1024, 4096], P(None, ('data', 'local'))
- w_down: bfloat16 [4, 4096, 1024], P(None, ('data', 'local'))
- lora_a: float32 [4, 1024, 4], replicated
- lora_b: float32 [4, 4, 4096], replicated
Outputs:
- output 1: bfloat16 [32768, 1024], P(('data', 'local'))
- output 2: bfloat16 [32768, 1024], P(('data', 'local'))
- output 3: float32 [4, 1024, 4], replicated
- output 4: float32 [4, 4, 4096], replicated
All inputs are finite; a program needn't handle non-finite values.
Results may differ from a plain program's by a relative error of at most 0.0186195.
Values are sent between devices in bfloat16 or wider.
A program may use at most 1 GiB of HBM per device.

v0:
```python
import jax
import jax.numpy as jnp
from jax import lax
from jax.sharding import PartitionSpec as P

GROUP = ("data", "local")
NORM_EPS = 1e-6
FULL_PRECISION = lax.Precision.HIGHEST


def gelu_tanh(pre_f):
    return jax.nn.gelu(pre_f, approximate=True)


def layer_forward(resid, full_up, full_down, adapt_a, adapt_b):
    resid_f = resid.astype(jnp.float32)
    inv_rms = lax.rsqrt(jnp.mean(resid_f * resid_f, axis=-1, keepdims=True) + NORM_EPS)
    normed = (resid_f * inv_rms).astype(jnp.bfloat16)
    low_rank = jnp.dot(normed, adapt_a, precision=FULL_PRECISION, preferred_element_type=jnp.float32)
    pre_act = (jnp.dot(normed, full_up, preferred_element_type=jnp.float32) + jnp.dot(low_rank, adapt_b, precision=FULL_PRECISION, preferred_element_type=jnp.float32)).astype(jnp.bfloat16)
    hidden_act = gelu_tanh(pre_act.astype(jnp.float32)).astype(jnp.bfloat16)
    new_resid = (resid_f + jnp.dot(hidden_act, full_down, preferred_element_type=jnp.float32)).astype(jnp.bfloat16)
    return new_resid, (resid, inv_rms, normed, low_rank, pre_act)


def layer_backward(d_resid, saved, full_up, full_down, adapt_a, adapt_b):
    resid, inv_rms, normed, low_rank, pre_act = saved
    d_hidden = jnp.einsum("th,fh->tf", d_resid, full_down, preferred_element_type=jnp.float32).astype(jnp.bfloat16)
    gelu_pull = jax.vjp(gelu_tanh, pre_act.astype(jnp.float32))[1]
    d_pre = gelu_pull(d_hidden.astype(jnp.float32))[0].astype(jnp.bfloat16)
    d_low = jnp.einsum("tf,rf->tr", d_pre, adapt_b, precision=FULL_PRECISION, preferred_element_type=jnp.float32)
    grad_b = jnp.einsum("tr,tf->rf", low_rank, d_pre, precision=FULL_PRECISION, preferred_element_type=jnp.float32)
    grad_a = jnp.einsum("th,tr->hr", normed, d_low, precision=FULL_PRECISION, preferred_element_type=jnp.float32)
    d_main = jnp.einsum("tf,hf->th", d_pre, full_up, preferred_element_type=jnp.float32).astype(jnp.bfloat16)
    d_side = jnp.einsum("tr,hr->th", d_low, adapt_a, precision=FULL_PRECISION, preferred_element_type=jnp.float32).astype(jnp.bfloat16)
    d_norm_f = (d_main + d_side).astype(jnp.float32)
    resid_f = resid.astype(jnp.float32)
    row_dot = jnp.mean(resid_f * d_norm_f, axis=-1, keepdims=True)
    d_resid_f = d_resid.astype(jnp.float32) + inv_rms * d_norm_f - resid_f * (inv_rms * inv_rms * inv_rms) * row_dot
    return d_resid_f.astype(jnp.bfloat16), grad_a, grad_b


def solution(mesh):
    data_size = mesh.shape["data"]
    tok_spec = P(GROUP, None)
    weight_spec = P(None, GROUP, None)

    def device_step(tokens, cotangent, up_shards, down_shards, value_a6, array_b6):
        local_idx = lax.axis_index("local")
        num_layers = up_shards.shape[0]
        up_rows = up_shards.shape[1] * data_size
        down_rows = down_shards.shape[1] * data_size
        resid = tokens
        kept = []
        for layer in range(num_layers):
            full_up = lax.all_gather(up_shards[layer], GROUP, axis=0, tiled=True)
            full_down = lax.all_gather(down_shards[layer], GROUP, axis=0, tiled=True)
            resid, saved = layer_forward(resid, full_up, full_down, value_a6[layer], array_b6[layer])
            keep_up = lax.dynamic_slice_in_dim(full_up, local_idx * up_rows, up_rows, axis=0)
            keep_down = lax.dynamic_slice_in_dim(full_down, local_idx * down_rows, down_rows, axis=0)
            kept.append((saved, keep_up, keep_down))
        d_resid = cotangent
        grads_a = []
        grads_b = []
        for layer in reversed(range(num_layers)):
            saved, keep_up, keep_down = kept[layer]
            full_up = lax.all_gather(keep_up, "local", axis=0, tiled=True)
            full_down = lax.all_gather(keep_down, "local", axis=0, tiled=True)
            d_resid, grad_a, grad_b = layer_backward(d_resid, saved, full_up, full_down, value_a6[layer], array_b6[layer])
            grad_a, grad_b = lax.psum((grad_a, grad_b), GROUP)
            grads_a.insert(0, grad_a)
            grads_b.insert(0, grad_b)
        return resid, d_resid, jnp.stack(grads_a), jnp.stack(grads_b)

    return jax.shard_map(device_step, mesh=mesh, in_specs=(tok_spec, tok_spec, weight_spec, weight_spec, P(), P()), out_specs=(tok_spec, tok_spec, P(), P()), check_vma=False)
```

profile of v0, /device:TPU:0, one launch (start us, length us, event | category | flops | bytes accessed | tf_op | source)
XLA Modules:
  0.0 1279.7 jit_solution(17694335707703133930)
XLA Ops:
  17.1 45.2 %all-gather.47.cloned.1.call-done = bf16[1,4096,1024]{2,1,0:T(8,128)(2,1)} async-done(((bf16[1,256,1024]{2,1,0:T(8,128)(2,1)}), bf16[1,4096,1024]{2,1,0:T(8,128)(2,1)}) %all-gather.47.cloned.1.call-update) | async-done | bytes 8388624 | tf_op jit(solution)/shard_map/all_gather | solution.py:57
  65.4 47.8 %all-gather.45.cloned.1.call-done = bf16[1,1024,4096]{2,1,0:T(8,128)(2,1)} async-done(((bf16[1,64,4096]{2,1,0:T(8,128)(2,1)}), bf16[1,1024,4096]{2,1,0:T(8,128)(2,1)}) %all-gather.45.cloned.1.call-update) | async-done | bytes 8388624 | tf_op jit(solution)/shard_map/all_gather | solution.py:56
  116.5 47.6 %all-gather.43.cloned.1.call-done = bf16[1,4096,1024]{2,1,0:T(8,128)(2,1)} async-done(((bf16[1,256,1024]{2,1,0:T(8,128)(2,1)}), bf16[1,4096,1024]{2,1,0:T(8,128)(2,1)}) %all-gather.43.cloned.1.call-update) | async-done | bytes 8388624 | tf_op jit(solution)/shard_map/all_gather | solution.py:57
  167.3 47.6 %all-gather.41.cloned.1.call-done = bf16[1,1024,4096]{2,1,0:T(8,128)(2,1)} async-done(((bf16[1,64,4096]{2,1,0:T(8,128)(2,1)}), bf16[1,1024,4096]{2,1,0:T(8,128)(2,1)}) %all-gather.41.cloned.1.call-update) | async-done | bytes 8388624 | tf_op jit(solution)/shard_map/all_gather | solution.py:56
  218.2 48.1 %all-gather.39.cloned.1.call-done = bf16[1,4096,1024]{2,1,0:T(8,128)(2,1)} async-done(((bf16[1,256,1024]{2,1,0:T(8,128)(2,1)}), bf16[1,4096,1024]{2,1,0:T(8,128)(2,1)}) %all-gather.39.cloned.1.call-update) | async-done | bytes 8388624 | tf_op jit(solution)/shard_map/all_gather | solution.py:57
  269.4 6.4 copy.10
  275.8 6.6 copy.12
  290.8 30.2 %fusion.174 = f32[2048,4096]{1,0:T(8,128)} fusion(f32[2048,4]{0,1:T(4,128)S(1)} %fusion.145, f32[4,4,4096]{2,1,0:T(4,128)S(1)} %copy-done.17), kind=kOutput, calls=%fused_computation.188 | convolution fusion | flops 402653184 | bytes 33652736 | tf_op jit(solution)/shard_map/dot_general | solution.py:20
  324.7 43.2 %all-gather.33.cloned.1.call-done = bf16[1,1024,4096]{2,1,0:T(8,128)(2,1)} async-done(((bf16[1,64,4096]{2,1,0:T(8,128)(2,1)}), bf16[1,1024,4096]{2,1,0:T(8,128)(2,1)}) %all-gather.33.cloned.1.call-update) | async-done | bytes 8388624 | tf_op jit(solution)/shard_map/all_gather | solution.py:56
  367.9 26.8 %add_convert_fusion.3 = bf16[2048,4096]{1,0:T(8,128)(2,1)} fusion(f32[2048,4096]{1,0:T(8,128)} %fusion.174, bf16[1,1024,4096]{2,1,0:T(8,128)(2,1)} %all-gather.33.cloned.1.call-done, bf16[2048,1024]{0,1:T(8,128)(2,1)} %copy.10, f32[2048]{0:T(1024)S(1)} %get-tuple-element.25), kind=kOutput, calls=%fused_computation.71 | convolution fusion | flops 17202937856 | bytes 62922752 | tf_op jit(solution)/shard_map/dot_general | solution.py:20
  394.7 24.1 %all-gather.35.cloned.1.call-done = bf16[1,4096,1024]{2,1,0:T(8,128)(2,1)} async-done(((bf16[1,256,1024]{2,1,0:T(8,128)(2,1)}), bf16[1,4096,1024]{2,1,0:T(8,128)(2,1)}) %all-gather.35.cloned.1.call-update) | async-done | bytes 8388624 | tf_op jit(solution)/shard_map/all_gather | solution.py:57
  418.8 25.7 %fusion.69 = (f32[2048]{0:T(1024)S(1)}, bf16[2048,1024]{0,1:T(8,128)(2,1)}) fusion(bf16[1,4096,1024]{2,1,0:T(8,128)(2,1)} %all-gather.35.cloned.1.call-done, bf16[2048,4096]{1,0:T(8,128)(2,1)} %add_convert_fusion.3, bf16[2048,1024]{0,1:T(8,128)(2,1)} %copy.10), kind=kOutput, calls=%fused_computation.117 | convolution fusion | flops 17276336128 | bytes 33562624 | tf_op jit(solution)/shard_map/dot_general | solution.py:22
  452.3 30.4 %fusion.170 = f32[2048,4096]{1,0:T(8,128)} fusion(f32[2048,4]{0,1:T(4,128)S(1)} %fusion.140, f32[4,4,4096]{2,1,0:T(4,128)S(1)} %copy-done.17), kind=kOutput, calls=%fused_computation.184 | convolution fusion | flops 402653184 | bytes 33652736 | tf_op jit(solution)/shard_map/dot_general | solution.py:20
  482.7 26.6 %add_convert_fusion.2 = bf16[2048,4096]{1,0:T(8,128)(2,1)} fusion(f32[2048,4096]{1,0:T(8,128)} %fusion.170, bf16[1,1024,4096]{2,1,0:T(8,128)(2,1)} %all-gather.37.cloned.1.call-done, bf16[2048,1024]{0,1:T(8,128)(2,1)S(1)} %copy-done.5, f32[2048]{0:T(1024)S(1)} %get-tuple-element.27), kind=kOutput, calls=%fused_computation.70 | convolution fusion | flops 17202937856 | bytes 62922752 | tf_op jit(solution)/shard_map/dot_general | solution.py:20
  509.4 25.8 %fusion.74 = (f32[2048]{0:T(1024)S(1)}, bf16[2048,1024]{0,1:T(8,128)(2,1)}) fusion(bf16[1,4096,1024]{2,1,0:T(8,128)(2,1)} %all-gather.39.cloned.1.call-done, bf16[2048,4096]{1,0:T(8,128)(2,1)} %add_convert_fusion.2, bf16[2048,1024]{0,1:T(8,128)(2,1)S(1)} %copy-done.5), kind=kOutput, calls=%fused_computation.122 | convolution fusion | flops 17276336128 | bytes 33562624 | tf_op jit(solution)/shard_map/dot_general | solution.py:22
  540.4 30.2 %fusion.166 = f32[2048,4096]{1,0:T(8,128)} fusion(f32[2048,4]{0,1:T(4,128)S(1)} %fusion.135, f32[4,4,4096]{2,1,0:T(4,128)S(1)} %copy-done.17), kind=kOutput, calls=%fused_computation.180 | convolution fusion | flops 402653184 | bytes 33652736 | tf_op jit(solution)/shard_map/dot_general | solution.py:20
  570.8 29.8 %add_convert_fusion.1 = bf16[2048,4096]{1,0:T(8,128)(2,1)} fusion(f32[2048,4096]{1,0:T(8,128)} %fusion.166, bf16[1,1024,4096]{2,1,0:T(8,128)(2,1)} %all-gather.41.cloned.1.call-done, bf16[2048,1024]{0,1:T(8,128)(2,1)} %get-tuple-element.35, f32[2048]{0:T(1024)S(1)} %get-tuple-element.29), kind=kOutput, calls=%fused_computation.69 | convolution fusion | flops 17202937856 | bytes 62922752 | tf_op jit(solution)/shard_map/dot_general | solution.py:20
  600.6 25.3 %fusion.79 = (f32[2048]{0:T(1024)S(1)}, bf16[2048,1024]{0,1:T(8,128)(2,1)}) fusion(bf16[1,4096,1024]{2,1,0:T(8,128)(2,1)} %all-gather.43.cloned.1.call-done, bf16[2048,4096]{1,0:T(8,128)(2,1)} %add_convert_fusion.1, bf16[2048,1024]{0,1:T(8,128)(2,1)S(1)} %copy-done.8), kind=kOutput, calls=%fused_computation.127 | convolution fusion | flops 17276336128 | bytes 33562624 | tf_op jit(solution)/shard_map/dot_general | solution.py:22
  630.6 30.7 %fusion.162 = f32[2048,4096]{1,0:T(8,128)} fusion(f32[2048,4]{0,1:T(4,128)S(1)} %fusion.130, f32[4,4,4096]{2,1,0:T(4,128)S(1)} %copy-done.17), kind=kOutput, calls=%fused_computation.176 | convolution fusion | flops 402653184 | bytes 33652736 | tf_op jit(solution)/shard_map/dot_general | solution.py:20
  661.3 26.6 %add_convert_fusion = bf16[2048,4096]{1,0:T(8,128)(2,1)} fusion(f32[2048,4096]{1,0:T(8,128)} %fusion.162, bf16[1,1024,4096]{2,1,0:T(8,128)(2,1)} %all-gather.45.cloned.1.call-done, bf16[2048,1024]{0,1:T(8,128)(2,1)S(1)} %copy-done.11, f32[2048]{0:T(1024)S(1)} %get-tuple-element.31), kind=kOutput, calls=%fused_computation.68 | convolution fusion | flops 17202937856 | bytes 62922752 | tf_op jit(solution)/shard_map/dot_general | solution.py:20
  687.9 25.0 %fusion.81 = bf16[2048,1024]{0,1:T(8,128)(2,1)} fusion(bf16[2048,1024]{0,1:T(8,128)(2,1)S(1)} %copy-done.11, bf16[1,4096,1024]{2,1,0:T(8,128)(2,1)} %all-gather.47.cloned.1.call-done, bf16[2048,4096]{1,0:T(8,128)(2,1)} %add_convert_fusion), kind=kOutput, calls=%fused_computation.129 | convolution fusion | flops 17270046720 | bytes 33554432 | tf_op jit(solution)/shard_map/dot_general | solution.py:22
  713.0 6.4 copy.14
  722.5 42.6 %fusion.15 = bf16[2048,4096]{1,0:T(8,128)(2,1)S(1)} fusion(bf16[2048,4096]{1,0:T(8,128)(2,1)} %add_convert_fusion, bf16[2048,1024]{1,0:T(8,128)(2,1)} %param.7, bf16[1,4096,1024]{2,1,0:T(8,128)(2,1)} %all-gather.49.cloned.1.call-done), kind=kOutput, calls=%fused_computation.38 | convolution fusion | flops 17372807168 | bytes 46137344 | tf_op jit(solution)/shard_map/th,fh->tf/dot_general | solution.py:28
  765.2 13.0 %fusion.160 = f32[2048,4]{0,1:T(4,128)S(1)} fusion(bf16[2048,4096]{1,0:T(8,128)(2,1)S(1)} %fusion.15, f32[4,4,4096]{2,1,0:T(4,128)S(1)} %copy-done.17), kind=kOutput, calls=%fused_computation.174 | convolution fusion | flops 402653184 | bytes 16875520 | tf_op jit(solution)/shard_map/tf,rf->tr/dot_general | solution.py:31
  778.8 8.4 fusion.184
  787.3 24.7 %fusion.83 = (f32[2048]{0:T(1024)S(1)}, bf16[2048,1024]{0,1:T(8,128)(2,1)S(1)}) fusion(bf16[2048,1024]{0,1:T(8,128)(2,1)} %get-tuple-element.37, bf16[2048,1024]{0,1:T(8,128)(2,1)} %fusion.184, bf16[2048,4096]{1,0:T(8,128)(2,1)} %copy-done.1, bf16[1,1024,4096]{2,1,0:T(8,128)(2,1)} %all-gather.51.cloned.1.call-done), kind=kOutput, calls=%fused_computation.131 | convolution fusion | flops 17192450048 | bytes 37756928 | tf_op jit(solution)/shard_map/tf,hf->th/dot_general | solution.py:34
  812.0 4.9 fusion.54
  816.9 46.7 %fusion.6 = bf16[2048,4096]{1,0:T(8,128)(2,1)S(1)} fusion(bf16[2048,4096]{1,0:T(8,128)(2,1)} %add_convert_fusion.1, bf16[2048,1024]{0,1:T(8,128)(2,1)} %fusion.54, bf16[1,4096,1024]{2,1,0:T(8,128)(2,1)} %all-gather.53.cloned.1.call-done), kind=kOutput, calls=%fused_computation.29 | convolution fusion | flops 17372807168 | bytes 46137344 | tf_op jit(solution)/shard_map/th,fh->tf/dot_general | solution.py:28
  863.7 13.0 %fusion.164 = f32[2048,4]{0,1:T(4,128)S(1)} fusion(bf16[2048,4096]{1,0:T(8,128)(2,1)S(1)} %fusion.6, f32[4,4,4096]{2,1,0:T(4,128)S(1)} %copy-done.17), kind=kOutput, calls=%fused_computation.178 | convolution fusion | flops 402653184 | bytes 16875520 | tf_op jit(solution)/shard_map/tf,rf->tr/dot_general | solution.py:31
  876.7 8.4 fusion.187
  885.1 24.7 %fusion.78 = (f32[2048]{0:T(1024)S(1)}, bf16[2048,1024]{0,1:T(8,128)(2,1)S(1)}) fusion(bf16[2048,1024]{0,1:T(8,128)(2,1)} %get-tuple-element.35, bf16[2048,1024]{0,1:T(8,128)(2,1)} %fusion.187, bf16[2048,4096]{1,0:T(8,128)(2,1)} %copy-done.2, bf16[1,1024,4096]{2,1,0:T(8,128)(2,1)} %all-gather.55.cloned.1.call-done), kind=kOutput, calls=%fused_computation.126 | convolution fusion | flops 17192450048 | bytes 37756928 | tf_op jit(solution)/shard_map/tf,hf->th/dot_general | solution.py:34
  914.8 46.7 %fusion.9 = bf16[2048,4096]{1,0:T(8,128)(2,1)S(1)} fusion(bf16[2048,4096]{1,0:T(8,128)(2,1)} %add_convert_fusion.2, bf16[2048,1024]{0,1:T(8,128)(2,1)} %fusion.57, bf16[1,4096,1024]{2,1,0:T(8,128)(2,1)} %all-gather.57.cloned.1.call-done), kind=kOutput, calls=%fused_computation.32 | convolution fusion | flops 17372807168 | bytes 46137344 | tf_op jit(solution)/shard_map/th,fh->tf/dot_general | solution.py:28
  961.6 13.0 %fusion.168 = f32[2048,4]{0,1:T(4,128)S(1)} fusion(bf16[2048,4096]{1,0:T(8,128)(2,1)S(1)} %fusion.9, f32[4,4,4096]{2,1,0:T(4,128)S(1)} %copy-done.17), kind=kOutput, calls=%fused_computation.182 | convolution fusion | flops 402653184 | bytes 16875520 | tf_op jit(solution)/shard_map/tf,rf->tr/dot_general | solution.py:31
  974.6 8.5 fusion.190
  995.1 24.5 %fusion.73 = (f32[2048]{0:T(1024)S(1)}, bf16[2048,1024]{0,1:T(8,128)(2,1)S(1)}) fusion(bf16[2048,1024]{0,1:T(8,128)(2,1)} %get-tuple-element.33, bf16[2048,1024]{0,1:T(8,128)(2,1)} %fusion.190, bf16[2048,4096]{1,0:T(8,128)(2,1)} %copy-done.3, bf16[1,1024,4096]{2,1,0:T(8,128)(2,1)} %all-gather.59.cloned.1.call-done), kind=kOutput, calls=%fused_computation.121 | convolution fusion | flops 17192450048 | bytes 37756928 | tf_op jit(solution)/shard_map/tf,hf->th/dot_general | solution.py:34
  1019.7 5.2 fusion.60
  1024.8 46.7 %fusion.12 = bf16[2048,4096]{1,0:T(8,128)(2,1)S(1)} fusion(bf16[2048,4096]{1,0:T(8,128)(2,1)} %add_convert_fusion.3, bf16[2048,1024]{0,1:T(8,128)(2,1)} %fusion.60, bf16[1,4096,1024]{2,1,0:T(8,128)(2,1)} %all-gather.61.cloned.1.call-done), kind=kOutput, calls=%fused_computation.35 | convolution fusion | flops 17372807168 | bytes 46137344 | tf_op jit(solution)/shard_map/th,fh->tf/dot_general | solution.py:28
  1071.6 13.0 %fusion.172 = f32[2048,4]{0,1:T(4,128)S(1)} fusion(bf16[2048,4096]{1,0:T(8,128)(2,1)S(1)} %fusion.12, f32[4,4,4096]{2,1,0:T(4,128)S(1)} %copy-done.17), kind=kOutput, calls=%fused_computation.186 | convolution fusion | flops 402653184 | bytes 16875520 | tf_op jit(solution)/shard_map/tf,rf->tr/dot_general | solution.py:31
  1088.6 8.5 fusion.193
  1097.2 10.9 convolution_bitcast_fusion.2
  1108.1 11.1 convolution_bitcast_fusion.1
  1119.3 7.2 convolution_bitcast_fusion
  1126.5 7.2 convolution_bitcast_fusion.3
  1133.8 25.6 %fusion.68 = (f32[2048]{0:T(1024)S(1)}, bf16[2048,1024]{0,1:T(8,128)(2,1)}) fusion(bf16[2048,1024]{0,1:T(8,128)(2,1)} %copy.10, bf16[2048,1024]{0,1:T(8,128)(2,1)} %fusion.193, bf16[2048,4096]{1,0:T(8,128)(2,1)} %copy-done.4, bf16[1,1024,4096]{2,1,0:T(8,128)(2,1)} %all-gather.63.cloned.1.call-done), kind=kOutput, calls=%fused_computation.116 | convolution fusion | flops 17192450048 | bytes 37756928 | tf_op jit(solution)/shard_map/tf,hf->th/dot_general | solution.py:34
  1159.5 7.8 fusion.63
  1167.3 6.4 copy.15
  1173.7 26.7 %all-reduce.5.cloned.1.call-done = (f32[1,1024,4]{1,2,0:T(4,128)}, f32[1,1024,4]{1,2,0:T(4,128)}, f32[1,1024,4]{1,2,0:T(4,128)}, f32[1,1024,4]{1,2,0:T(4,128)}) async-done(((f32[1,1024,4]{1,2,0:T(4,128)}, f32[1,1024,4]{1,2,0:T(4,128)}, f32[1,1024,4]{1,2,0:T(4,128)}, f32[1,1024,4]{1,2,0:T(4,128)}), (f32[1,1024,4]{1,2,0:T(4,128)}, f32[1,1024,4]{1,2,0:T(4,128)}, f32[1,1024,4]{1,2,0:T(4,128)}, ...) | async-done | bytes 65552 | tf_op jit(solution)/shard_map/psum | solution.py:70
  1201.8 69.0 %all-reduce.7.cloned.1.call-done = (f32[1,4,4096]{2,1,0:T(4,128)}, f32[1,4,4096]{2,1,0:T(4,128)}, f32[1,4,4096]{2,1,0:T(4,128)}, f32[1,4,4096]{2,1,0:T(4,128)}) async-done(((f32[1,4,4096]{2,1,0:T(4,128)}, f32[1,4,4096]{2,1,0:T(4,128)}, f32[1,4,4096]{2,1,0:T(4,128)}, f32[1,4,4096]{2,1,0:T(4,128)}), (f32[1,4,4096]{2,1,0:T(4,128)}, f32[1,4,4096]{2,1,0:T(4,128)}, f32[1,4,4096]{2,1,0:T(4,128)}, ...) | async-done | bytes 262160 | tf_op jit(solution)/shard_map/psum | solution.py:70
  (177 shorter events, 83.5 us)
Async XLA Ops:
  7.2 55.1 %all-gather.47.cloned.1.call-start = ((), (), s32[]{:S(2)}) async-start(), calls=%async_computation.7 | async-start | bytes 8912896 | tf_op jit(solution)/shard_map/all_gather | solution.py:57
  10.1 103.1 %all-gather.45.cloned.1.call-start = ((), (), s32[]{:S(2)}) async-start(), calls=%async_computation.6 | async-start | bytes 8912896 | tf_op jit(solution)/shard_map/all_gather | solution.py:56
  13.0 151.1 %all-gather.43.cloned.1.call-start = ((), (), s32[]{:S(2)}) async-start(), calls=%async_computation.5 | async-start | bytes 8912896 | tf_op jit(solution)/shard_map/all_gather | solution.py:57
  13.8 201.1 %all-gather.41.cloned.1.call-start = ((), (), s32[]{:S(2)}) async-start(), calls=%async_computation.4 | async-start | bytes 8912896 | tf_op jit(solution)/shard_map/all_gather | solution.py:56
  14.3 251.9 %all-gather.39.cloned.1.call-start = ((), (), s32[]{:S(2)}) async-start(), calls=%async_computation.3 | async-start | bytes 8912896 | tf_op jit(solution)/shard_map/all_gather | solution.py:57
  14.9 306.1 %all-gather.37.cloned.1.call-start = ((), (), s32[]{:S(2)}) async-start(), calls=%async_computation.2 | async-start | bytes 8912896 | tf_op jit(solution)/shard_map/all_gather | solution.py:56
  15.5 352.4 %all-gather.33.cloned.1.call-start = ((), (), s32[]{:S(2)}) async-start(), calls=%async_computation | async-start | bytes 8912896 | tf_op jit(solution)/shard_map/all_gather | solution.py:56
  16.3 402.6 %all-gather.35.cloned.1.call-start = ((), (), s32[]{:S(2)}) async-start(), calls=%async_computation.1 | async-start | bytes 8912896 | tf_op jit(solution)/shard_map/all_gather | solution.py:57
  17.0 705.5 %all-gather.49.cloned.1.call-start = ((), (), s32[]{:S(2)}) async-start(), calls=%async_computation.8 | async-start | bytes 10485760 | tf_op jit(solution)/shard_map/all_gather | solution.py:68
  65.4 721.9 %all-gather.51.cloned.1.call-start = ((), (), s32[]{:S(2)}) async-start(), calls=%async_computation.9 | async-start | bytes 10485760 | tf_op jit(solution)/shard_map/all_gather | solution.py:67
  116.5 700.4 %all-gather.53.cloned.1.call-start = ((), (), s32[]{:S(2)}) async-start(), calls=%async_computation.10 | async-start | bytes 10485760 | tf_op jit(solution)/shard_map/all_gather | solution.py:68
  167.2 717.9 %all-gather.55.cloned.1.call-start = ((), (), s32[]{:S(2)}) async-start(), calls=%async_computation.11 | async-start | bytes 10485760 | tf_op jit(solution)/shard_map/all_gather | solution.py:67
  218.1 696.7 %all-gather.57.cloned.1.call-start = ((), (), s32[]{:S(2)}) async-start(), calls=%async_computation.12 | async-start | bytes 10485760 | tf_op jit(solution)/shard_map/all_gather | solution.py:68
  269.3 725.8 %all-gather.59.cloned.1.call-start = ((), (), s32[]{:S(2)}) async-start(), calls=%async_computation.13 | async-start | bytes 10485760 | tf_op jit(solution)/shard_map/all_gather | solution.py:67
  286.1 81.8 %copy-start.29 = (f32[2048]{0:T(1024)}, f32[2048]{0:T(1024)S(1)}, u32[]{:S(2)}) copy-start(f32[2048]{0:T(1024)S(1)} %get-tuple-element.25) | copy-start | bytes 24580
  324.2 700.6 %all-gather.61.cloned.1.call-start = ((), (), s32[]{:S(2)}) async-start(), calls=%async_computation.14 | async-start | bytes 10485760 | tf_op jit(solution)/shard_map/all_gather | solution.py:68
  448.2 34.5 %copy-start.31 = (f32[2048]{0:T(1024)}, f32[2048]{0:T(1024)S(1)}, u32[]{:S(2)}) copy-start(f32[2048]{0:T(1024)S(1)} %get-tuple-element.27) | copy-start | bytes 24580
  452.3 30.4 %copy-start.22 = (f32[2048,4]{0,1:T(4,128)}, f32[2048,4]{0,1:T(4,128)S(1)}, u32[]{:S(2)}) copy-start(f32[2048,4]{0,1:T(4,128)S(1)} %fusion.140) | copy-start | bytes 98308
  452.3 30.4 %copy-start.5 = (bf16[2048,1024]{0,1:T(8,128)(2,1)S(1)}, bf16[2048,1024]{0,1:T(8,128)(2,1)}, u32[]{:S(2)}) copy-start(bf16[2048,1024]{0,1:T(8,128)(2,1)} %get-tuple-element.33) | copy-start | bytes 12582916
  535.8 35.0 %copy-start.33 = (f32[2048]{0:T(1024)}, f32[2048]{0:T(1024)S(1)}, u32[]{:S(2)}) copy-start(f32[2048]{0:T(1024)S(1)} %get-tuple-element.29) | copy-start | bytes 24580
  570.7 563.1 %all-gather.63.cloned.1.call-start = ((), (), s32[]{:S(2)}) async-start(), calls=%async_computation.15 | async-start | bytes 10485760 | tf_op jit(solution)/shard_map/all_gather | solution.py:67
  570.8 29.9 %copy-start.8 = (bf16[2048,1024]{0,1:T(8,128)(2,1)S(1)}, bf16[2048,1024]{0,1:T(8,128)(2,1)}, u32[]{:S(2)}) copy-start(bf16[2048,1024]{0,1:T(8,128)(2,1)} %get-tuple-element.35) | copy-start | bytes 12582916
  626.6 34.7 %copy-start.35 = (f32[2048]{0:T(1024)}, f32[2048]{0:T(1024)S(1)}, u32[]{:S(2)}) copy-start(f32[2048]{0:T(1024)S(1)} %get-tuple-element.31) | copy-start | bytes 24580
  630.6 30.7 %copy-start.26 = (f32[2048,4]{0,1:T(4,128)}, f32[2048,4]{0,1:T(4,128)S(1)}, u32[]{:S(2)}) copy-start(f32[2048,4]{0,1:T(4,128)S(1)} %fusion.130) | copy-start | bytes 98308
  630.6 30.7 %copy-start.11 = (bf16[2048,1024]{0,1:T(8,128)(2,1)S(1)}, bf16[2048,1024]{0,1:T(8,128)(2,1)}, u32[]{:S(2)}) copy-start(bf16[2048,1024]{0,1:T(8,128)(2,1)} %get-tuple-element.37) | copy-start | bytes 12582916
  722.5 477.9 %all-reduce.5.cloned.1.call-start = ((), (), s32[]{:S(2)}) async-start(), calls=%async_computation.16 | async-start | bytes 131072 | tf_op jit(solution)/shard_map/psum | solution.py:70
  787.2 24.7 %copy-start.36 = (f32[2048]{0:T(1024)S(1)}, f32[2048]{0:T(1024)}, u32[]{:S(2)}) copy-start(f32[2048]{0:T(1024)} %copy-done.35) | copy-start | bytes 24580
  787.2 24.7 %copy-start.41 = (f32[2048]{0:T(1024)S(1)}, f32[2048]{0:T(1024)}, u32[]{:S(2)}) copy-start(f32[2048]{0:T(1024)} %get-tuple-element.30) | copy-start | bytes 24580
  787.2 24.7 %copy-start.12 = (bf16[2048,1024]{0,1:T(8,128)(2,1)S(1)}, bf16[2048,1024]{0,1:T(8,128)(2,1)}, u32[]{:S(2)}) copy-start(bf16[2048,1024]{0,1:T(8,128)(2,1)} %get-tuple-element.37) | copy-start | bytes 12582916
  787.2 24.7 %copy-start.16 = (bf16[2048,1024]{0,1:T(8,128)(2,1)S(1)}, bf16[2048,1024]{0,1:T(8,128)(2,1)}, u32[]{:S(2)}) copy-start(bf16[2048,1024]{0,1:T(8,128)(2,1)} %copy.12) | copy-start | bytes 12582916
  885.1 24.7 %copy-start.34 = (f32[2048]{0:T(1024)S(1)}, f32[2048]{0:T(1024)}, u32[]{:S(2)}) copy-start(f32[2048]{0:T(1024)} %copy-done.33) | copy-start | bytes 24580
  885.1 24.7 %copy-start.40 = (f32[2048]{0:T(1024)S(1)}, f32[2048]{0:T(1024)}, u32[]{:S(2)}) copy-start(f32[2048]{0:T(1024)} %get-tuple-element.28) | copy-start | bytes 24580
  885.1 24.7 %copy-start.9 = (bf16[2048,1024]{0,1:T(8,128)(2,1)S(1)}, bf16[2048,1024]{0,1:T(8,128)(2,1)}, u32[]{:S(2)}) copy-start(bf16[2048,1024]{0,1:T(8,128)(2,1)} %get-tuple-element.35) | copy-start | bytes 12582916
  885.1 24.8 %copy-start.15 = (bf16[2048,1024]{0,1:T(8,128)(2,1)S(1)}, bf16[2048,1024]{0,1:T(8,128)(2,1)}, u32[]{:S(2)}) copy-start(bf16[2048,1024]{0,1:T(8,128)(2,1)} %fusion.54) | copy-start | bytes 12582916
  961.5 21.6 %copy-start.6 = (bf16[2048,1024]{0,1:T(8,128)(2,1)S(1)}, bf16[2048,1024]{0,1:T(8,128)(2,1)}, u32[]{:S(2)}) copy-start(bf16[2048,1024]{0,1:T(8,128)(2,1)} %get-tuple-element.33) | copy-start | bytes 12582916
  961.5 21.6 %copy-start.32 = (f32[2048]{0:T(1024)S(1)}, f32[2048]{0:T(1024)}, u32[]{:S(2)}) copy-start(f32[2048]{0:T(1024)} %copy-done.31) | copy-start | bytes 24580
  974.6 16.5 %copy-start.13 = (bf16[2048,1024]{0,1:T(8,128)(2,1)S(1)}, bf16[2048,1024]{0,1:T(8,128)(2,1)}, u32[]{:S(2)}) copy-start(bf16[2048,1024]{0,1:T(8,128)(2,1)} %get-tuple-element.37) | copy-start | bytes 12582916
  974.6 16.5 %copy-start.19 = (f32[2048,4]{0,1:T(4,128)S(1)}, f32[2048,4]{0,1:T(4,128)}, u32[]{:S(2)}) copy-start(f32[2048,4]{0,1:T(4,128)} %copy-done.18) | copy-start | bytes 98308
  974.6 16.5 %copy-start.37 = (f32[2048]{0:T(1024)S(1)}, f32[2048]{0:T(1024)}, u32[]{:S(2)}) copy-start(f32[2048]{0:T(1024)} %copy-done.35) | copy-start | bytes 24580
  995.1 24.5 %copy-start.39 = (f32[2048]{0:T(1024)S(1)}, f32[2048]{0:T(1024)}, u32[]{:S(2)}) copy-start(f32[2048]{0:T(1024)} %get-tuple-element.26) | copy-start | bytes 24580
  995.1 24.5 %copy-start.7 = (bf16[2048,1024]{0,1:T(8,128)(2,1)S(1)}, bf16[2048,1024]{0,1:T(8,128)(2,1)}, u32[]{:S(2)}) copy-start(bf16[2048,1024]{0,1:T(8,128)(2,1)} %get-tuple-element.33) | copy-start | bytes 12582916
  995.1 24.6 %copy-start.14 = (bf16[2048,1024]{0,1:T(8,128)(2,1)S(1)}, bf16[2048,1024]{0,1:T(8,128)(2,1)}, u32[]{:S(2)}) copy-start(bf16[2048,1024]{0,1:T(8,128)(2,1)} %fusion.57) | copy-start | bytes 12582916
  1097.2 22.0 %slice-start = ((s8[16777216]{0:T(1024)(128)(4,1)}), s8[4194304]{0:T(1024)(128)(4,1)S(1)}, s32[]{:S(2)}) async-start(s8[16777216]{0:T(1024)(128)(4,1)} %bitcast.175), calls=%async_computation.18 | async-start | bytes 8388608
  1097.2 22.0 %slice-start.1 = ((s8[16777216]{0:T(1024)(128)(4,1)}), s8[4194304]{0:T(1024)(128)(4,1)S(1)}, s32[]{:S(2)}) async-start(s8[16777216]{0:T(1024)(128)(4,1)} %bitcast.175), calls=%async_computation.19 | async-start | bytes 8388608
  1108.1 18.4 %slice-start.4 = ((s8[16777216]{0:T(1024)(128)(4,1)}), s8[4194304]{0:T(1024)(128)(4,1)S(1)}, s32[]{:S(2)}) async-start(s8[16777216]{0:T(1024)(128)(4,1)} %bitcast.177), calls=%async_computation.22 | async-start | bytes 8388608
  1108.1 18.4 %slice-start.5 = ((s8[16777216]{0:T(1024)(128)(4,1)}), s8[4194304]{0:T(1024)(128)(4,1)S(1)}, s32[]{:S(2)}) async-start(s8[16777216]{0:T(1024)(128)(4,1)} %bitcast.177), calls=%async_computation.23 | async-start | bytes 8388608
  1133.8 25.7 %copy-start.38 = (f32[2048]{0:T(1024)S(1)}, f32[2048]{0:T(1024)}, u32[]{:S(2)}) copy-start(f32[2048]{0:T(1024)} %get-tuple-element.24) | copy-start | bytes 24580
  1133.8 137.0 %all-reduce.7.cloned.1.call-start = ((), (), s32[]{:S(2)}) async-start(), calls=%async_computation.17 | async-start | bytes 524288 | tf_op jit(solution)/shard_map/psum | solution.py:70
  (20 other events, 196.6 us)
Sparse Core Ops, SparseCore 0:
  10.8 51.4 all-gather.46
  64.5 48.6 all-gather.44
  115.4 48.6 all-gather.42
  166.2 48.6 all-gather.40
  217.6 48.6 all-gather.38
  268.3 48.6 all-gather.36
  319.2 48.6 all-gather.32
  370.1 48.6 all-gather.34
  420.6 83.6 all-gather.48
  505.9 83.6 all-gather.50
  591.4 83.6 all-gather.52
  676.7 83.6 all-gather.54
  762.2 83.6 all-gather.56
  847.5 83.6 all-gather.58
  932.8 83.6 all-gather.60
  1018.2 83.6 all-gather.62
  1133.9 66.4 all-reduce.4
  1205.6 65.0 all-reduce.6
where the time goes:
time: 1290 us; the launch traced here: 1280 us
  matrix products  770 us (60%)
  waiting for transfers between devices  403 us (31%)
  local copies, waits for them, and re-layouts  58.6 us (5%)
  other arithmetic  31.4 us (2%)
  between operations  15.3 us (1%)
    dot_general x4, matrix products, layer_backward(): jnp.einsum('th,fh->tf', d_resid, full_down, preferred_element_type=jnp.fl...  183 us
    all_gather x4, waiting for transfers between devices, device_step(): full_down = lax.all_gather(down_shards[layer], GROUP, axis=0, tiled=True)  165 us
    all_gather x4, waiting for transfers between devices, device_step(): full_up = lax.all_gather(up_shards[layer], GROUP, axis=0, tiled=True)  139 us
    dot_general x4, matrix products, layer_forward(): jnp.dot(low_rank, adapt_b, precision=FULL_PRECISION, preferred_element_ty...  122 us
    dot_general x4, matrix products, layer_forward(): jnp.dot(normed, full_up, preferred_element_type=jnp.float32)  110 us
    dot_general x4, matrix products, layer_forward(): jnp.dot(hidden_act, full_down, preferred_element_type=jnp.float32)  102 us
    dot_general x4, matrix products, layer_backward(): jnp.einsum('tf,hf->th', d_pre, full_up, preferred_element_type=jnp.float32)  99.5 us
    psum x2, waiting for transfers between devices, device_step(): grad_a, grad_b = lax.psum((grad_a, grad_b), GROUP)  95.7 us
  transfers between devices with their start and end apart: 18, of which 9 were waited for; matrix products, arithmetic and copies ran while one was open for 67% of the time, Pallas kernels for 0%

commit v1 on v0

v1 whole, which is shorter than its diff:
```python
import jax
import jax.numpy as jnp
from jax import lax
from jax.experimental import pallas as pl
from jax.experimental.pallas import tpu as pltpu
from jax.sharding import PartitionSpec as P

GROUP = ("data", "local")
NORM_EPS = 1e-6
BF = jnp.bfloat16
F32 = jnp.float32
C0 = 0.7978845608028654
K0 = 0.044715

T = 2048
H = 1024
F = 4096
L = 4
NG = 8 * L
MU = 512
MD = 1024
ROWS = ((0, 96), (96, 80), (176, 80))
GW = 640


def nn(a, b):
    return lax.dot_general(a, b, (((1,), (0,)), ((), ())), preferred_element_type=F32)


def nt(a, b):
    return lax.dot_general(a, b, (((1,), (1,)), ((), ())), preferred_element_type=F32)


def tn(a, b):
    return lax.dot_general(a, b, (((0,), (0,)), ((), ())), preferred_element_type=F32)


def split3(v):
    p1 = v.astype(BF).astype(F32)
    rest = v - p1
    p2 = rest.astype(BF).astype(F32)
    return p1, p2, (rest - p2).astype(BF).astype(F32)


def left_parts(v):
    p1, p2, p3 = split3(v)
    return jnp.concatenate([p1, p2, p3, p1, p1, p2], axis=0).astype(BF)


def right_parts(v):
    p1, p2, p3 = split3(v)
    return jnp.concatenate([p3, p2, p1, p1, p2, p1], axis=0).astype(BF)


def sum_parts(v):
    return v[0:8] + v[8:16] + v[16:24]


def gelu_and_slope(pre):
    x = pre.astype(F32)
    sq = x * x
    half = 0.5 * jnp.tanh(x * (sq * (C0 * K0) + C0)) + 0.5
    act = x * half
    slope = (act * (1.0 - half)) * (sq * (6.0 * C0 * K0) + 2.0 * C0) + half
    return act.astype(BF), slope


def rows_of(m, size):
    return pl.ds(pl.multiple_of(m * size, size), size)


def kernel(
    tok, cot, up, down, a8, b8,
    xout, gtok, gout, gp, xs, kept,
    w, sd, xb, ub, db, gst, acat, bcat, vcat, dcat, dlt, gb, ga, gacc, rbuf, gall,
    own_sem, fs_sem, fr_sem, kept_sem, gp_sem, io_sem, bo_sem, bs_sem, br_sem, rs_sem, rr_sem, as_sem, ar_sem,
    cred,
):
    data = lax.axis_index("data")
    local = lax.axis_index("local")
    x, c = lax.div(data, 2), lax.rem(data, 2)
    z, y = lax.div(local, 2), lax.rem(local, 2)
    me = data * 4 + local
    dx, dy, dz, dc = 1 - 2 * x, 1 - 2 * y, 1 - 2 * z, 1 - 2 * c
    par = lax.rem(x + y + z, 2)

    def quarter(i):
        hi, lo = lax.div(i, 2), lax.rem(i, 2)
        return 2 * (par + hi - 2 * par * hi) + (c + lo - 2 * c * lo)

    q_own, q_miss = quarter(0), quarter(2)

    def pick(dim, a0, a1, a2):
        return lax.div((1 - dim) * (2 - dim), 2) * a0 + dim * (2 - dim) * a1 + lax.div(dim * (dim - 1), 2) * a2

    def device(dim):
        return (local + pick(dim, 0, dy, 2 * dz), data + pick(dim, 2 * dx, 0, 0))

    neighbours = ((local, data + 2 * dx), (local + dy, data), (local + 2 * dz, data), (local, data + dc))
    partner = neighbours[3]

    def remote(src, dst, ssem, rsem, dev):
        return pltpu.make_async_remote_copy(
            src_ref=src, dst_ref=dst, send_sem=ssem, recv_sem=rsem, device_id=dev, device_id_type=pl.DeviceIdType.MESH
        )


    def own_load(g):
        s, l = lax.rem(g, 8), lax.div(g, 8)

        @pl.when(s < 4)
        def _():
            for n in range(4):
                pltpu.make_async_copy(
                    up.at[l, :, pl.ds(pl.multiple_of(s * 1024 + n * 256, 256), 256)],
                    w.at[s, me, pl.ds(n * 64, 64), :],
                    own_sem.at[s],
                ).start()

        @pl.when(s >= 4)
        def _():
            pltpu.make_async_copy(
                down.at[l, :, pl.ds(pl.multiple_of((s - 4) * 256, 256), 256)], w.at[s, me], own_sem.at[s]
            ).start()

    def colour(g):
        q = lax.rem(g + c, 3)
        return q, lax.rem(q + 2, 3), lax.rem(q + 1, 3)

    def delta(dim):
        return pick(dim, 8 * dx, dy, 2 * dz)

    def use_credit(g, dim):
        @pl.when(g >= 8)
        def _():
            pl.semaphore_wait(cred.at[dim, lax.rem(g, 8)], 1)

    def send_blocks(g, phase, dim, blocks, dev):
        s = lax.rem(g, 8)
        use_credit(g, dim)
        for b in blocks:
            remote(w.at[s, b], w.at[s, b], fs_sem.at[phase, s], fr_sem.at[phase, s], dev).start()

    def span(g, phase):
        s = lax.rem(g, 8)
        r = w.at[s, pl.ds(0, (1, 2, 4, 8)[phase])]
        return remote(r, r, fs_sem.at[phase, s], fr_sem.at[phase, s], partner)

    def ready(g):
        return jnp.logical_and(g >= 0, g < NG)

    def event0(r):
        g3, g6 = r + 3, r + 6

        @pl.when(ready(g3))
        def _():
            d1, d2, d3 = colour(g3)
            e1, e2 = delta(d1), delta(d2)
            span(g3, 1).wait_recv()
            send_blocks(g3, 2, d3, (me, me + e1, me + e2, me + e1 + e2), device(d3))

        @pl.when(ready(g6))
        def _():
            d1, _, _ = colour(g6)
            s = lax.rem(g6, 8)
            pltpu.make_async_copy(w.at[s, me], w.at[s, me], own_sem.at[s]).wait()
            send_blocks(g6, 0, d1, (me,), device(d1))

    def event1(r):
        g5, g2 = r + 5, r + 2

        @pl.when(ready(g5))
        def _():
            d1, d2, _ = colour(g5)
            span(g5, 0).wait_recv()
            send_blocks(g5, 1, d2, (me, me + delta(d1)), device(d2))

        @pl.when(ready(g2))
        def _():
            s = lax.rem(g2, 8)
            span(g2, 2).wait_recv()
            use_credit(g2, 3)
            for h in range(2):
                r2 = w.at[s, pl.ds(8 * h + 4 * c, 4)]
                remote(r2, r2, fs_sem.at[3, s], fr_sem.at[3, s], partner).start()

    def keep_copy(g):
        s, l = lax.rem(g, 8), lax.div(g, 8)
        return pltpu.make_async_copy(w.at[s, pl.ds(4 * q_own, 4)], kept.at[l, s], kept_sem.at[s])

    def arrive(g):
        span(g, 3).wait_recv()
        keep_copy(g).start()

    def release(g):
        s = lax.rem(g, 8)
        for phase in range(4):
            span(g, phase).wait_send()
        keep_copy(g).wait()
        for i in range(4):
            pl.semaphore_signal(cred.at[i, s], inc=1, device_id=neighbours[i], device_id_type=pl.DeviceIdType.MESH)

        @pl.when(g + 8 < NG)
        def _():
            own_load(g + 8)


    def whole(m, q):
        return w.at[pl.ds(4 * m, 4), pl.ds(4 * q, 4)]

    def part(ref, dim):
        return ref.at[:, :, pl.ds(*ROWS[dim]), :]

    def b_own(m, l):
        return pltpu.make_async_copy(kept.at[l, pl.ds(4 * m, 4)], whole(m, q_own), bo_sem.at[m])

    def b_send(m, l, i, q):
        src, dst = kept.at[l, pl.ds(4 * m, 4)], whole(m, q)
        if i < 3:
            src, dst = part(src, i), part(dst, i)
        return remote(src, dst, bs_sem.at[m, i], br_sem.at[m, i], neighbours[i])

    def b_forward(m):
        return remote(whole(m, q_miss), whole(m, q_miss), bs_sem.at[m, 4], br_sem.at[m, 4], partner)

    def gather(m, l):
        b_own(m, l).start()
        for i in range(4):
            for s in range(4):
                pl.semaphore_wait(cred.at[i, 4 * m + s], 1)
            b_send(m, l, i, q_own).start()

    def b_events(m, l, i):
        @pl.when(i == 0)
        def _():
            b_own(m, l).wait()

        @pl.when(i == 1)
        def _():
            b_send(m, l, 3, quarter(1)).wait_recv()

        @pl.when(i == 2)
        def _():
            for d in range(3):
                b_send(m, l, d, q_miss).wait_recv()
            b_forward(m).start()

        @pl.when(i == 3)
        def _():
            b_forward(m).wait_recv()

    def b_release(m, l):
        b_forward(m).wait_send()
        for i in range(4):
            b_send(m, l, i, q_own).wait_send()

        @pl.when(l > 0)
        def _():
            for i in range(4):
                for s in range(4):
                    pl.semaphore_signal(
                        cred.at[i, 4 * m + s], inc=1, device_id=neighbours[i], device_id_type=pl.DeviceIdType.MESH
                    )


    def grad_send(l, i):
        return remote(
            gacc.at[l, :, pl.ds(i * GW, GW)], rbuf.at[me], rs_sem.at[l], rr_sem, (jnp.int32(i), l)
        )

    def grads_out(l):
        for i in range(4):
            mine = me == 4 * l + i

            @pl.when(jnp.logical_not(mine))
            def _():
                grad_send(l, i).start()

            @pl.when(mine)
            def _():
                rbuf[me] = gacc[l, :, i * GW : (i + 1) * GW]


    tok_in = pltpu.make_async_copy(tok, xb, io_sem.at[0])
    cot_in = pltpu.make_async_copy(cot, db, io_sem.at[1])

    def first_loads(g, _):
        own_load(g)
        return 0

    lax.fori_loop(0, 8, first_loads, 0)
    tok_in.start()
    cot_in.start()

    def fill(r, _):
        event0(r)
        event1(r)
        return 0

    for l in range(L):
        acat[l] = right_parts(a8[l])
        bcat[l] = right_parts(b8[l])
    lax.fori_loop(-6, 0, fill, 0)
    tok_in.wait()
    cot_in.wait()


    def inv_rms(rf):
        return lax.rsqrt(jnp.mean(rf * rf, axis=-1, keepdims=True) + NORM_EPS)

    def x_save(l):
        return pltpu.make_async_copy(xb, xs.at[l - 1], io_sem.at[0])

    def gp_out(l, k, m):
        b = lax.rem(m, 2)
        return pltpu.make_async_copy(gst.at[b], gp.at[l, k, rows_of(m, MU), :], gp_sem.at[b])

    def forward_layer(l, _):
        @pl.when(l > 0)
        def _():
            x_save(l).start()

        def prep(m, _):
            r = rows_of(m, MU)
            rf = xb[r, :].astype(F32)
            u = (rf * inv_rms(rf)).astype(BF)
            ub[r, :] = u
            vcat[l, :, r] = left_parts(sum_parts(nt(acat[l, 0:32], u)))
            return 0

        lax.fori_loop(0, T // MU, prep, 0)

        def up_chunk(k, _):
            g = 8 * l + k

            def tile(m, _):
                @pl.when(m == 0)
                def _():
                    event0(g)
                    arrive(g)

                @pl.when(m == 2)
                def _():
                    event1(g)

                @pl.when(g * 4 + m - 16 * l >= 2)
                def _():
                    gp_out(l, k, m).wait()

                r = rows_of(m, MU)
                for n in range(4):
                    cols = pl.ds(pl.multiple_of(k * 1024 + n * 256, 256), 256)
                    rhs = w[k, :, n * 64 : (n + 1) * 64, :].reshape(H, 256)
                    pre = nn(ub[r, :], rhs) + tn(vcat[l, :, r], bcat[l, :, cols])
                    act, slope = gelu_and_slope(pre.astype(BF))
                    sd[r, cols] = act
                    gst[lax.rem(m, 2), :, n * 256 : (n + 1) * 256] = slope
                gp_out(l, k, m).start()
                return 0

            lax.fori_loop(0, T // MU, tile, 0)
            release(g)
            return 0

        lax.fori_loop(0, 4, up_chunk, 0)

        @pl.when(l > 0)
        def _():
            x_save(l).wait()

        def down_chunk(k, _):
            g = 8 * l + 4 + k

            def tile(m, _):
                @pl.when(m == 0)
                def _():
                    event0(g)
                    arrive(g)

                @pl.when(m == 1)
                def _():
                    event1(g)

                r = rows_of(m, MD)
                cols = pl.ds(pl.multiple_of(k * 256, 256), 256)
                step = nn(sd[r, :], w[4 + k].reshape(F, 256))
                xb[r, cols] = (xb[r, cols].astype(F32) + step).astype(BF)
                return 0

            lax.fori_loop(0, T // MD, tile, 0)
            release(g)
            return 0

        lax.fori_loop(0, 4, down_chunk, 0)
        return 0

    lax.fori_loop(0, L, forward_layer, 0)


    x_final = pltpu.make_async_copy(xb, xout, io_sem.at[0])
    x_final.start()
    gather(1, L - 1)
    gp_out(L - 1, 3, 2).wait()
    gp_out(L - 1, 3, 3).wait()

    def gp_in(t):
        l = L - 1 - lax.div(t, 16)
        q = quarter(lax.div(lax.rem(t, 16), 4))
        m = lax.rem(t, 4)
        b = lax.rem(m, 2)
        return pltpu.make_async_copy(gp.at[l, q, rows_of(m, MU), :], gst.at[b], gp_sem.at[b])

    gp_in(jnp.int32(0)).start()
    x_final.wait()


    def x_load(l, start):
        @pl.when(l > 0)
        def _():
            cp = pltpu.make_async_copy(xs.at[l - 1], xb, io_sem.at[0])
            cp.start() if start else cp.wait()

        @pl.when(l == 0)
        def _():
            cp = pltpu.make_async_copy(tok, xb, io_sem.at[0])
            cp.start() if start else cp.wait()

    def backward_layer(rl, _):
        l = L - 1 - rl
        x_load(l, True)
        dlt[...] = jnp.zeros_like(dlt)
        gb[...] = jnp.zeros_like(gb)
        ga[...] = jnp.zeros_like(ga)

        def down_step(i, _):
            @pl.when(i == 0)
            def _():
                gather(0, l)

            b_events(1, l, i)
            q = quarter(i)
            cols = pl.ds(pl.multiple_of(q * 1024, 1024), 1024)

            def tile(m, _):
                t = rl * 16 + i * 4 + m

                @pl.when(t + 1 < 16 * L)
                def _():
                    gp_in(t + 1).start()

                gp_in(t).wait()
                r = rows_of(m, MU)
                acc = None
                for k in range(4):
                    rhs = w[4 + k, pl.ds(4 * q, 4)].reshape(1024, 256)
                    term = nt(db[r, k * 256 : (k + 1) * 256], rhs)
                    acc = term if acc is None else acc + term
                d = (acc.astype(BF).astype(F32) * gst[lax.rem(m, 2)]).astype(BF)
                sd[r, cols] = d
                dlt[:, r] += nt(bcat[l, 0:32, cols], d)
                gb[:, cols] += nn(vcat[l, 0:32, r], d)
                return 0

            lax.fori_loop(0, T // MU, tile, 0)
            return 0

        lax.fori_loop(0, 4, down_step, 0)
        b_release(1, l)
        dcat[...] = left_parts(sum_parts(dlt[...]))
        gb8 = sum_parts(gb[...])
        gacc[l, :, 0:2048] = gb8[:, 0:2048] + pltpu.roll(gb8[:, 2048:4096], 4, 0)

        def up_step(i, _):
            @pl.when(jnp.logical_and(i == 0, l > 0))
            def _():
                gather(1, l - 1)

            b_events(0, l, i)
            q = quarter(i)
            cols = pl.ds(pl.multiple_of(q * 256, 256), 256)

            def tile(m, _):
                r = rows_of(m, MD)
                acc = None
                for k in range(4):
                    for n in range(4):
                        rhs = w[k, pl.ds(4 * q, 4), n * 64 : (n + 1) * 64, :].reshape(256, 256)
                        j = 4 * k + n
                        term = nt(sd[r, j * 256 : (j + 1) * 256], rhs)
                        acc = term if acc is None else acc + term
                side = tn(dcat[:, r], acat[l, :, cols]).astype(BF)
                ub[r, cols] = acc.astype(BF) + side
                return 0

            lax.fori_loop(0, T // MD, tile, 0)
            return 0

        lax.fori_loop(0, 4, up_step, 0)
        b_release(0, l)
        x_load(l, False)

        def finish(m, _):
            r = rows_of(m, MU)
            rf = xb[r, :].astype(F32)
            inv = inv_rms(rf)
            dn = ub[r, :].astype(F32)
            dot = jnp.mean(rf * dn, axis=-1, keepdims=True)
            db[r, :] = (db[r, :].astype(F32) + inv * dn - rf * (inv * inv * inv) * dot).astype(BF)
            u = (rf * inv).astype(BF)
            ga[...] += nn(dcat[0:32, r], u)
            return 0

        lax.fori_loop(0, T // MU, finish, 0)
        ga8 = sum_parts(ga[...])
        gacc[l, :, 2048:2560] = ga8[:, 0:512] + pltpu.roll(ga8[:, 512:1024], 4, 0)
        grads_out(l)
        return 0

    lax.fori_loop(0, L, backward_layer, 0)


    g_final = pltpu.make_async_copy(db, gtok, io_sem.at[1])
    g_final.start()
    for l in range(L):
        for i in range(4):

            @pl.when(me != 4 * l + i)
            def _():
                grad_send(jnp.int32(l), i).wait_send()

    others = rbuf.at[pl.ds(0, 15)]
    remote(others, others, rr_sem, rr_sem, partner).wait_recv()
    total = rbuf[0]
    for i in range(1, 16):
        total = total + rbuf[i]
    gall[me] = total

    def share(o, _):
        @pl.when(o != me)
        def _():
            remote(gall.at[me], gall.at[me], as_sem, ar_sem, (lax.rem(o, 4), lax.div(o, 4))).start()

        return 0

    lax.fori_loop(0, 16, share, 0)
    others = gall.at[pl.ds(0, 15)]
    remote(others, others, as_sem, ar_sem, partner).wait_send()
    remote(others, others, as_sem, ar_sem, partner).wait_recv()
    gout[...] = gall[...]
    g_final.wait()


def solution(mesh):
    tok_spec = P(GROUP, None)
    weight_spec = P(None, GROUP, None)

    def device_step(tokens, cotangent, up, down, lora_a, lora_b):
        a8 = jnp.pad(lora_a.transpose(0, 2, 1), ((0, 0), (0, 4), (0, 0)))
        b8 = jnp.pad(lora_b, ((0, 0), (0, 4), (0, 0)))
        hbm = pl.BlockSpec(memory_space=pltpu.HBM)
        vmem = pl.BlockSpec(memory_space=pltpu.VMEM)
        shape = jax.ShapeDtypeStruct
        dma, regular = pltpu.SemaphoreType.DMA, pltpu.SemaphoreType.REGULAR
        outs = pl.pallas_call(
            kernel,
            name="stack",
            out_shape=[
                shape((T, H), BF),
                shape((T, H), BF),
                shape((16, 8, GW), F32),
                shape((L, 4, T, 1024), F32),
                shape((L - 1, T, H), BF),
                shape((L, 8, 4, 256, 256), BF),
            ],
            in_specs=[hbm, hbm, hbm, hbm, vmem, vmem],
            out_specs=[hbm, hbm, vmem, hbm, hbm, hbm],
            scratch_shapes=[
                pltpu.VMEM((8, 16, 256, 256), BF),
                pltpu.VMEM((T, F), BF),
                pltpu.VMEM((T, H), BF),
                pltpu.VMEM((T, H), BF),
                pltpu.VMEM((T, H), BF),
                pltpu.VMEM((2, MU, 1024), F32),
                pltpu.VMEM((L, 48, H), BF),
                pltpu.VMEM((L, 48, F), BF),
                pltpu.VMEM((L, 48, T), BF),
                pltpu.VMEM((48, T), BF),
                pltpu.VMEM((32, T), F32),
                pltpu.VMEM((32, F), F32),
                pltpu.VMEM((32, H), F32),
                pltpu.VMEM((L, 8, 4 * GW), F32),
                pltpu.VMEM((16, 8, GW), F32),
                pltpu.VMEM((16, 8, GW), F32),
                dma((8,)),
                dma((4, 8)),
                dma((4, 8)),
                dma((8,)),
                dma((2,)),
                dma((2,)),
                dma((2,)),
                dma((2, 5)),
                dma((2, 5)),
                dma((L,)),
                dma,
                dma,
                dma,
                regular((4, 8)),
            ],
            compiler_params=pltpu.CompilerParams(vmem_limit_bytes=67000000, has_side_effects=True),
        )(tokens, cotangent, up, down, a8, b8)
        x_out, g_tok, shares = outs[:3]
        grads = shares.reshape(L, 4, 2, 4, GW).transpose(0, 2, 3, 1, 4).reshape(L, 2, 4, 4 * GW)
        grad_b = grads[..., 0:2048].transpose(0, 2, 1, 3).reshape(L, 4, F)
        grad_a = grads[..., 2048:2560].transpose(0, 1, 3, 2).reshape(L, H, 4)
        return x_out, g_tok, grad_a, grad_b

    return jax.shard_map(
        device_step,
        mesh=mesh,
        in_specs=(tok_spec, tok_spec, weight_spec, weight_spec, P(), P()),
        out_specs=(tok_spec, tok_spec, P(), P()),
        check_vma=False,
    )
```

time: 1290 us -> 554 us (0.43)
  matrix products: 770 us -> 0 us
  Pallas kernels: 0 us -> 540 us
  waiting for transfers between devices: 403 us -> 0 us
  local copies, waits for them, and re-layouts: 58.6 us -> 12.8 us
  other arithmetic: 31.4 us -> 0 us
  between operations: 15.3 us -> 0.66 us
    dot_general x40 -> x0, matrix products: 770 us -> none  [the longest x4 183 us: layer_backward(): jnp.einsum('th,fh->tf', d_resid, full_down, preferred_element_type=jnp.fl...]
    pallas_call x0 -> x1, Pallas kernels: none -> 540 us  [device_step(): pl.pallas_call(kernel, name='stack', out_shape=[shape((T, H), BF), shape(...]
    all_gather x16 -> x0, waiting for transfers between devices: 304 us -> none  [the longest x4 165 us: device_step(): full_down = lax.all_gather(down_shards[layer], GROUP, axis=0, tiled=True)]
    psum x2 -> x0, waiting for transfers between devices: 95.7 us -> none  [device_step(): grad_a, grad_b = lax.psum((grad_a, grad_b), GROUP)]
    dynamic_slice x8 -> x0, local copies, waits for them, and re-layouts: 25 us -> none  [the longest x4 12.7 us: device_step(): lax.dynamic_slice_in_dim(full_up, local_idx * up_rows, up_rows, axis=0)]
    convert_element_type x4 -> x0, other arithmetic: 22.8 us -> none  [layer_backward(): return (d_resid_f.astype(jnp.bfloat16), grad_a, grad_b)]
    unnamed x104 -> x4, local copies, waits for them, and re-layouts: 27.9 us -> 6.83 us
  transfers between devices with their start and end apart: 18 -> 0, of which waited for: 9 -> 0; matrix products, arithmetic and copies ran while one was open for 67% -> 0% of each run, Pallas kernels for 0% -> 0%
where the time goes in v1:
time: 554 us
  Pallas kernels  540 us (97%)
  local copies, waits for them, and re-layouts  12.8 us (2%)
    pallas_call x1, Pallas kernels, device_step(): pl.pallas_call(kernel, name='stack', out_shape=[shape((T, H), BF), shape(...  540 us

profile of v1, /device:TPU:0, one launch (start us, length us, event | category | flops | bytes accessed | tf_op | source)
XLA Modules:
  0.0 553.8 jit_solution(17631891927519588797)
XLA Ops:
  0.6 1.5 pad.8.a8
  2.1 1.8 pad.9.b8
  3.9 540.4 %stack.1 = (bf16[2048,1024]{1,0:T(8,128)(2,1)}, bf16[2048,1024]{1,0:T(8,128)(2,1)}, f32[16,8,640]{2,1,0:T(8,128)}, f32[4,4,2048,1024]{3,2,1,0:T(8,128)}, bf16[3,...) custom-call(bf16[2048,1024]{1,0:T(8,128)(2,1)} %tok.1, bf16[2048,1024]{1,0:T(8,128)(2,1)} %cot.1, ...), custom_call_target="tpu_custom_call" | custom-call | tf_op jit(solution)/shard_map/stack/pallas_call | solution.py:564
  544.3 1.1 reshape.20
  545.4 0.1 copy.12
  545.5 0.2 reshape.21
  545.7 0.6 slice.8
  546.3 0.7 slice.9
  547.0 0.0 copy-start
  547.0 4.8 copy.15
  551.8 0.0 copy-done
  551.8 2.0 copy.16
Async XLA Ops:
  547.0 4.8 copy-start
